TPU v7x, 32 devices: a whole 2x2x4 slice. The times are simulated.
32 devices in a mesh: dp: 8 (over z, x), seq: 4 (over y, core).
Axes of the slice: x: 2, y: 2, z: 4, core: 2. Of those that a mesh axis runs over, the one named last changes fastest.
Arguments:
- hidden: bfloat16 [8, 4096, 4096], P('dp', 'seq'), may hold values from -6 to 6
- value_weight: bfloat16 [4096, 64], replicated, may hold values from -0.09375 to 0.09375
- value_bias: float32 [64], replicated, may hold values from -1 to 1
- returns: float32 [8, 4096], P('dp', 'seq'), may hold values from -12 to 12, as said below
- task_bins: int32 [8, 4096], P('dp', 'seq'), may hold values from 0 to 63
- loss_mask: int32 [8, 4096], P('dp', 'seq'), may hold values 0 or 1
Outputs:
- targets: float32 [8, 4096], P('dp', 'seq')
- weight_grad: float32 [4096, 64], replicated
- bias_grad: float32 [64], replicated
Inputs may be any that keep to these rules, and one draw needn't show every extreme that they name: The returns of one rollout share a level and a trend along positions.
All inputs are finite; a program needn't handle non-finite values.
Results may differ from a plain program's by a relative error of at most 0.00083.
Values sent between devices are 32-bit elements.
No kernel may reach another device: no remote copies, remote signals or barrier semaphores. Data moves between devices by JAX's collectives and lax.ppermute only.
A program may use at most 64 MiB of HBM per device.

v0:
```python
import jax
import jax.numpy as jnp
from jax import lax
from jax.sharding import PartitionSpec as P


def on_device(hidden, value_weight, value_bias, returns, task_bins, loss_mask):
    rollouts = hidden.shape[0] * lax.axis_size("dp")
    states = hidden.reshape(-1, hidden.shape[2])
    flat_returns = returns.reshape(-1)
    bins_iota = jnp.arange(value_weight.shape[1], dtype=jnp.int32)
    chosen = (task_bins.reshape(-1)[:, None] == bins_iota).astype(jnp.float32)
    valid = loss_mask.reshape(-1).astype(jnp.float32)
    onehot = chosen * valid[:, None]
    scores = jnp.dot(states, value_weight, preferred_element_type=jnp.float32)
    counts = jnp.sum(onehot, axis=0)
    summed = jnp.sum(onehot * flat_returns[:, None], axis=0)
    squares = jnp.sum(onehot * flat_returns[:, None] * flat_returns[:, None], axis=0)
    counts, summed, squares = lax.psum((counts, summed, squares), ("dp", "seq"))
    means = summed / jnp.maximum(counts, 1.0)
    second = squares - summed * means
    floor_counts = jnp.maximum(counts, 1.0)
    spread = jnp.sqrt(second / floor_counts + 0.1)
    deviation = flat_returns[:, None] - means
    targets = jnp.sum(chosen * (deviation / spread), axis=-1)
    predicted = jnp.sum((scores + value_bias) * chosen, axis=-1)
    slope = valid * jnp.clip(predicted - targets, -1.0, 1.0) / rollouts
    coefficient = chosen * slope[:, None]
    weight_grad = lax.dot_general(
        states,
        coefficient.astype(jnp.bfloat16),
        (((0,), (0,)), ((), ())),
        preferred_element_type=jnp.float32,
    )
    bias_grad = jnp.sum(coefficient, axis=0)
    weight_grad, bias_grad = lax.psum((weight_grad, bias_grad), ("dp", "seq"))
    return (targets.reshape(returns.shape), weight_grad, bias_grad)


def solution(mesh):
    placed = (P("dp", "seq", None), P(), P(), P("dp", "seq"), P("dp", "seq"), P("dp", "seq"))
    return jax.shard_map(
        on_device, mesh=mesh, in_specs=placed, out_specs=(P("dp", "seq"), P(), P()), check_vma=False
    )
```

profile of v0, /device:TPU:0, one launch (start us, length us, event | category | flops | bytes accessed | tf_op | source)
XLA Modules:
  0.0 201.0 jit_solution(13949442704553326158)
XLA Ops:
  7.2 0.0 copy-start
  7.2 0.0 copy-start.2
  7.2 0.0 all-reduce.3.cloned.1.call-start
  7.2 0.7 convert_element_type.17
  8.0 0.9 fusion.17
  8.9 42.0 %all-reduce = (f32[64]{0:T(128)S(1)}, f32[64]{0:T(128)S(1)}, f32[64]{0:T(128)S(1)}) all-reduce(f32[64]{0:T(128)S(1)} %get-tuple-element.4, f32[64]{0:T(128)S(1)} %get-tuple-element.3, f32[64]{0:T(128)S(1)} %get-tuple-element.5), channel_id=1, replica_groups=mesh['dp'=8,'seq'=4] {'dp','seq'}, use_global_device_ids=true, to_apply=%region_5.0 | all-reduce | flops 192 | bytes 1536 | tf_op jit(solution)/shard_map/psum | solution.py:19
  50.9 0.0 copy-start.1
  50.9 1.0 select_reduce_fusion.2
  51.9 0.0 copy-done
  51.9 0.0 copy-start.3
  51.9 6.3 %fusion.13 = f32[1024]{0:T(1024)S(1)} fusion(bf16[4096,64]{0,1:T(8,128)(2,1)S(1)} %copy-done, bf16[1,1024,4096]{2,1,0:T(8,128)(2,1)} %param.6, f32[64]{0:T(128)} %param.8, s32[1024]{0:T(1024)} %bitcast.22), kind=kOutput, calls=%fused_computation.7 | convolution fusion | flops 537132032 | bytes 8921344 | tf_op jit(solution)/shard_map/dot_general | solution.py:15
  58.2 0.0 copy-done.2
  58.2 0.0 copy-done.1
  58.3 2.5 %fusion.4 = f32[4096,64]{0,1:T(8,128)} fusion(bf16[1,1024,4096]{2,1,0:T(8,128)(2,1)S(1)} %copy-done.1, f32[1024]{0:T(1024)S(1)} %multiply_multiply_fusion, s32[1024]{0:T(1024)S(1)} %bitcast.23), kind=kOutput, calls=%fused_computation.4 | convolution fusion | flops 537001984 | bytes 9445376 | tf_op jit(solution)/shard_map/dot_general | solution.py:29
  60.8 0.0 copy-done.3
  60.8 0.0 all-reduce.3.cloned.1.call-update
  60.8 0.1 select_reduce_fusion
  61.0 40.3 %psum.39 = f32[64]{0:T(128)} all-reduce(f32[64]{0:T(128)S(1)} %select_reduce_fusion), channel_id=1, replica_groups=mesh['dp'=8,'seq'=4] {'dp','seq'}, use_global_device_ids=true, to_apply=%region_10.11 | all-reduce | flops 64 | bytes 512 | tf_op jit(solution)/shard_map/psum | solution.py:36
  101.3 90.6 %all-reduce.3.cloned.1.call-done = f32[4096,64]{0,1:T(8,128)} async-done(((f32[4096,64]{0,1:T(8,128)}), f32[4096,64]{0,1:T(8,128)}) %all-reduce.3.cloned.1.call-update) | async-done | bytes 1048592 | tf_op jit(solution)/shard_map/psum | solution.py:36
  191.9 2.3 %copy.10 = f32[4096,64]{0,1:T(8,128)} copy(f32[4096,64]{0,1:T(8,128)} %all-reduce.3.cloned.1.call-done) | data formatting | bytes 2097152
  (2 shorter events, 0.0 us)
Async XLA Ops:
  7.2 44.8 %copy-start = (bf16[4096,64]{0,1:T(8,128)(2,1)S(1)}, bf16[4096,64]{0,1:T(8,128)(2,1)}, u32[]{:S(2)}) copy-start(bf16[4096,64]{0,1:T(8,128)(2,1)} %param.7) | copy-start | bytes 1572868
  7.2 51.1 %copy-start.2 = (s32[1,1024]{1,0:T(1,128)S(1)}, s32[1,1024]{1,0:T(1,128)}, u32[]{:S(2)}) copy-start(s32[1,1024]{1,0:T(1,128)} %param.10) | copy-start | bytes 12292
  7.2 184.7 %all-reduce.3.cloned.1.call-start = ((), (), s32[]{:S(2)}) async-start(), calls=%async_computation | async-start | bytes 2097152 | tf_op jit(solution)/shard_map/psum | solution.py:36
  50.9 7.3 %copy-start.1 = (bf16[1,1024,4096]{2,1,0:T(8,128)(2,1)S(1)}, bf16[1,1024,4096]{2,1,0:T(8,128)(2,1)}, u32[]{:S(2)}) copy-start(bf16[1,1024,4096]{2,1,0:T(8,128)(2,1)} %param.6) | copy-start | bytes 25165828
  51.9 8.9 %copy-start.3 = (f32[1024]{0:T(1024)}, f32[1024]{0:T(1024)S(1)}, u32[]{:S(2)}) copy-start(f32[1024]{0:T(1024)S(1)} %select_reduce_fusion.2) | copy-start | bytes 12292
Sparse Core Ops, SparseCore 0:
  60.9 130.8 all-reduce.2
where the time goes:
time: 202 us; the launch traced here: 201 us
  waiting for transfers between devices  90.6 us (45%)
  blocking collectives  82.4 us (41%)
  between operations  14.1 us (7%)
  matrix products  8.82 us (4%)
  other arithmetic  2.77 us (1%)
  local copies, waits for them, and re-layouts  2.3 us (1%)
    psum x1, waiting for transfers between devices, on_device(): weight_grad, bias_grad = lax.psum((weight_grad, bias_grad), ('dp', 'seq'))  90.6 us
    psum x1, blocking collectives, on_device(): counts, summed, squares = lax.psum((counts, summed, squares), ('dp', 'seq'))  42 us
    psum x1, blocking collectives, on_device(): weight_grad, bias_grad = lax.psum((weight_grad, bias_grad), ('dp', 'seq'))  40.3 us
    dot_general x1, matrix products, on_device(): scores = jnp.dot(states, value_weight, preferred_element_type=jnp.float32)  6.27 us
  transfers between devices with their start and end apart: 1, of which 1 were waited for; matrix products, arithmetic and copies ran while one was open for 0% of the time, Pallas kernels for 0%

commit v1 on v0

--- a/solution.py
+++ b/solution.py
@@ -2,6 +2,11 @@
 import jax.numpy as jnp
 from jax import lax
 from jax.sharding import PartitionSpec as P
+
+
+def axis_by_axis(value, one, other):
+    inner = lax.psum(value, one)
+    return lax.psum(inner, other)
 
 
 def on_device(hidden, value_weight, value_bias, returns, task_bins, loss_mask):
@@ -33,7 +38,7 @@
         preferred_element_type=jnp.float32,
     )
     bias_grad = jnp.sum(coefficient, axis=0)
-    weight_grad, bias_grad = lax.psum((weight_grad, bias_grad), ("dp", "seq"))
+    weight_grad, bias_grad = axis_by_axis((weight_grad, bias_grad), "dp", "seq")
     return (targets.reshape(returns.shape), weight_grad, bias_grad)
 
 

time: 202 us -> 187 us (0.926)
  blocking collectives: 82.4 us -> 68.2 us
    psum x1 -> x2, blocking collectives: 40.3 us -> 26.2 us  [the longest x1 20 us: axis_by_axis(): inner = lax.psum(value, one)]
    psum x1 -> x2, waiting for transfers between devices: 90.6 us -> 90 us  [the longest x1 78 us: axis_by_axis(): inner = lax.psum(value, one)]
  transfers between devices with their start and end apart: 1 -> 2, of which waited for: 1 -> 2; matrix products, arithmetic and copies ran while one was open for 0% -> 0% of each run, Pallas kernels for 0% -> 0%
where the time goes in v1:
time: 187 us; the launch traced here: 186 us
  waiting for transfers between devices  90 us (48%)
  blocking collectives  68.2 us (36%)
  between operations  14.1 us (8%)
  matrix products  8.82 us (5%)
  other arithmetic  2.77 us (1%)
  local copies, waits for them, and re-layouts  2.3 us (1%)
    psum x1, waiting for transfers between devices, axis_by_axis(): inner = lax.psum(value, one)  78 us
    psum x1, blocking collectives, on_device(): counts, summed, squares = lax.psum((counts, summed, squares), ('dp', 'seq'))  42 us
    psum x1, blocking collectives, axis_by_axis(): inner = lax.psum(value, one)  20 us
    psum x1, waiting for transfers between devices, axis_by_axis(): return lax.psum(inner, other)  12 us
    dot_general x1, matrix products, on_device(): scores = jnp.dot(states, value_weight, preferred_element_type=jnp.float32)  6.27 us
    psum x1, blocking collectives, axis_by_axis(): return lax.psum(inner, other)  6.15 us
  transfers between devices with their start and end apart: 2, of which 2 were waited for; matrix products, arithmetic and copies ran while one was open for 0% of the time, Pallas kernels for 0%

profile of v1, /device:TPU:0, one launch (start us, length us, event | category | flops | bytes accessed | tf_op | source)
XLA Modules:
  0.0 186.3 jit_solution(14436269642975887312)
XLA Ops:
  7.2 0.0 copy-start
  7.2 0.0 copy-start.2
  7.2 0.0 all-reduce.4.cloned.1.call-start
  7.2 0.7 convert_element_type.17
  8.0 0.9 fusion.17
  8.9 42.0 %all-reduce = (f32[64]{0:T(128)S(1)}, f32[64]{0:T(128)S(1)}, f32[64]{0:T(128)S(1)}) all-reduce(f32[64]{0:T(128)S(1)} %get-tuple-element.4, f32[64]{0:T(128)S(1)} %get-tuple-element.3, f32[64]{0:T(128)S(1)} %get-tuple-element.5), channel_id=1, replica_groups=mesh['dp'=8,'seq'=4] {'dp','seq'}, use_global_device_ids=true, to_apply=%region_5.0 | all-reduce | flops 192 | bytes 1536 | tf_op jit(solution)/shard_map/psum | solution.py:24
  50.9 0.0 copy-start.1
  50.9 1.0 select_reduce_fusion.2
  51.9 0.0 copy-done
  51.9 0.0 copy-start.3
  51.9 6.3 %fusion.13 = f32[1024]{0:T(1024)S(1)} fusion(bf16[4096,64]{0,1:T(8,128)(2,1)S(1)} %copy-done, bf16[1,1024,4096]{2,1,0:T(8,128)(2,1)} %param.6, f32[64]{0:T(128)} %param.8, s32[1024]{0:T(1024)} %bitcast.22), kind=kOutput, calls=%fused_computation.7 | convolution fusion | flops 537132032 | bytes 8921344 | tf_op jit(solution)/shard_map/dot_general | solution.py:20
  58.2 0.0 copy-done.2
  58.2 0.0 copy-done.1
  58.3 2.5 %fusion.4 = f32[4096,64]{0,1:T(8,128)} fusion(bf16[1,1024,4096]{2,1,0:T(8,128)(2,1)S(1)} %copy-done.1, f32[1024]{0:T(1024)S(1)} %multiply_multiply_fusion, s32[1024]{0:T(1024)S(1)} %bitcast.23), kind=kOutput, calls=%fused_computation.4 | convolution fusion | flops 537001984 | bytes 9445376 | tf_op jit(solution)/shard_map/dot_general | solution.py:34
  60.8 0.0 copy-done.3
  60.8 0.0 all-reduce.4.cloned.1.call-update
  60.8 0.0 all-reduce.6.cloned.1.call-start
  60.9 78.0 %all-reduce.4.cloned.1.call-done = f32[4096,64]{0,1:T(8,128)} async-done(((f32[4096,64]{0,1:T(8,128)}), f32[4096,64]{0,1:T(8,128)}) %all-reduce.4.cloned.1.call-update) | async-done | bytes 1048592 | tf_op jit(solution)/shard_map/psum | solution.py:8
  138.9 0.0 all-reduce.6.cloned.1.call-update
  138.9 0.1 select_reduce_fusion
  139.1 20.0 %psum.54 = f32[64]{0:T(128)S(1)} all-reduce(f32[64]{0:T(128)S(1)} %select_reduce_fusion), channel_id=1, replica_groups=mesh['dp'=8,'seq'=4] {'dp'}, use_global_device_ids=true, to_apply=%region_11.12 | all-reduce | flops 64 | bytes 512 | tf_op jit(solution)/shard_map/psum | solution.py:8
  159.1 6.2 %psum.55 = f32[64]{0:T(128)} all-reduce(f32[64]{0:T(128)S(1)} %psum.54), channel_id=1, replica_groups=mesh['dp'=8,'seq'=4] {'seq'}, use_global_device_ids=true, to_apply=%region_12.13 | all-reduce | flops 64 | bytes 512 | tf_op jit(solution)/shard_map/psum | solution.py:9
  165.3 12.0 %all-reduce.6.cloned.1.call-done = f32[4096,64]{0,1:T(8,128)} async-done(((f32[4096,64]{0,1:T(8,128)}), f32[4096,64]{0,1:T(8,128)}) %all-reduce.6.cloned.1.call-update) | async-done | bytes 1048592 | tf_op jit(solution)/shard_map/psum | solution.py:9
  177.2 2.3 %copy.11 = f32[4096,64]{0,1:T(8,128)} copy(f32[4096,64]{0,1:T(8,128)} %all-reduce.6.cloned.1.call-done) | data formatting | bytes 2097152
  (2 shorter events, 0.0 us)
Async XLA Ops:
  7.2 44.8 %copy-start = (bf16[4096,64]{0,1:T(8,128)(2,1)S(1)}, bf16[4096,64]{0,1:T(8,128)(2,1)}, u32[]{:S(2)}) copy-start(bf16[4096,64]{0,1:T(8,128)(2,1)} %param.7) | copy-start | bytes 1572868
  7.2 51.1 %copy-start.2 = (s32[1,1024]{1,0:T(1,128)S(1)}, s32[1,1024]{1,0:T(1,128)}, u32[]{:S(2)}) copy-start(s32[1,1024]{1,0:T(1,128)} %param.10) | copy-start | bytes 12292
  7.2 131.7 %all-reduce.4.cloned.1.call-start = ((), (), s32[]{:S(2)}) async-start(), calls=%async_computation | async-start | bytes 2097152 | tf_op jit(solution)/shard_map/psum | solution.py:8
  50.9 7.3 %copy-start.1 = (bf16[1,1024,4096]{2,1,0:T(8,128)(2,1)S(1)}, bf16[1,1024,4096]{2,1,0:T(8,128)(2,1)}, u32[]{:S(2)}) copy-start(bf16[1,1024,4096]{2,1,0:T(8,128)(2,1)} %param.6) | copy-start | bytes 25165828
  51.9 8.9 %copy-start.3 = (f32[1024]{0:T(1024)}, f32[1024]{0:T(1024)S(1)}, u32[]{:S(2)}) copy-start(f32[1024]{0:T(1024)S(1)} %select_reduce_fusion.2) | copy-start | bytes 12292
  60.8 116.4 %all-reduce.6.cloned.1.call-start = ((), (), s32[]{:S(2)}) async-start(), calls=%async_computation.1 | async-start | bytes 2097152 | tf_op jit(solution)/shard_map/psum | solution.py:9
Sparse Core Ops, SparseCore 0:
  60.9 77.9 all-reduce.3
  141.3 35.8 all-reduce.5
